TPU v7x, 32 devices: a whole 2x2x4 slice. The times are simulated.
32 devices in a mesh: dp: 2 (over y), ctx: 4 (over z), tp: 4 (over x, core).
Axes of the slice: x: 2, y: 2, z: 4, core: 2. Of those that a mesh axis runs over, the one named last changes fastest.
Arguments:
- layer_input: bfloat16 [2, 512, 8192], P('dp', 'ctx'), may hold values from -6 to 6
- queries: bfloat16 [2, 512, 16384], P('dp', 'ctx', 'tp'), may hold values from -6 to 6
- key_heads: bfloat16 [2, 512, 1024], P('dp', 'ctx', 'tp'), may hold values from -6 to 6
- value_heads: bfloat16 [2, 512, 1024], P('dp', 'ctx', 'tp'), may hold values from -6 to 6
- attn_out: bfloat16 [2, 512, 16384], P('dp', 'ctx', 'tp'), may hold values from -6 to 6
- out_grad: bfloat16 [2, 512, 16384], P('dp', 'ctx', 'tp'), may hold values from -6 to 6
- log_sums: float32 [2, 128, 512], P('dp', 'tp', 'ctx'), may hold values from 4 to 7
- doc_ids: int32 [2, 512], P('dp'), may hold values from 0 to 7, never falling along the last dimension, each value on 1 to 193 neighbouring positions
Outputs:
- query_grad: bfloat16 [2, 512, 16384], P('dp', 'ctx', 'tp')
- key_grad: bfloat16 [2, 512, 1024], P('dp', 'ctx', 'tp')
- value_grad: bfloat16 [2, 512, 1024], P('dp', 'ctx', 'tp')
- weight_grad: float32 [8192, 1024], P(('dp', 'ctx'), 'tp')
Inputs may be any that keep to these rules, and one draw needn't show every extreme that they name: `doc_ids`: along each sequence's positions the document ids never fall; every id names 1 to 193 positions, and one names exactly 193.
All inputs are finite; a program needn't handle non-finite values.
Results may differ from a plain program's by a relative error of at most 0.0061.
Values may be sent and summed in bfloat16 or wider, within the bound.
A program may use at most 64 MiB of HBM per device.

v0:
```python
import functools
import jax
import jax.numpy as jnp
from jax import lax
from jax.experimental import pallas as pl
from jax.experimental.pallas import tpu as pltpu
from jax.sharding import PartitionSpec as P

REACH = 4
HD = 128
LANES = 128
CORES = 2
MESH = pl.DeviceIdType.MESH
F32 = jnp.float32
BF16 = jnp.bfloat16


def contract(left, right, dims):
    return lax.dot_general(left, right, (dims, ((), ())), preferred_element_type=F32)


def place_of(block, count):
    return jnp.where(block < count, block, 2 * count - 1 - block), jnp.where(block < count, 0, 1)


def fused_kernel(
    sizes,
    layer_hbm,
    q_hbm,
    k_hbm,
    v_hbm,
    o_hbm,
    do_hbm,
    lse_ref,
    doc_ref,
    dq_hbm,
    dk_ref,
    dv_ref,
    w_hbm,
    q_s,
    o_s,
    do_s,
    dq_s,
    kbuf,
    vbuf,
    bias_s,
    lse_s,
    dkv_s,
    acc_s,
    send_s,
    recv_s,
    a_s,
    at_s,
    vg_s,
    w_s,
    load_sem,
    own_sem,
    kv_send,
    kv_recv,
    g_send,
    g_recv,
    a_send,
    a_recv,
    x_send,
    x_recv,
    c_send,
    c_recv,
    vg_send,
    vg_recv,
    out_sem,
):
    ndp, n, ntp = sizes
    dp, me, tp = lax.axis_index("dp"), lax.axis_index("ctx"), lax.axis_index("tp")
    rows = q_s.shape[0]
    block = rows // 2
    groups = k_hbm.shape[2] // HD
    per_group = q_s.shape[1] // HD // groups
    stack = 2 * LANES // block
    span = REACH * block
    width = groups * HD
    scale = HD ** (-0.5)
    feats = w_s.shape[0]
    xs = ntp // CORES
    core = lax.rem(tp, CORES)
    chip = tp // CORES
    strip = rows // ntp
    own_row = pl.multiple_of((core * xs + chip) * strip, strip)
    core_row = pl.multiple_of(core * xs * strip, strip)
    others = [(a, b) for a in range(ndp) for b in range(n) if (a, b) != (0, 0)]
    others.sort(key=lambda ab: (ab[1] != 0, ab[0] + min(ab[1], n - ab[1])))
    blocks = (me, 2 * n - 1 - me)

    def peer(shift):
        return lax.rem(dp + shift[0], ndp), lax.rem(me + shift[1], n)

    def source(shift):
        return lax.rem(dp + ndp - shift[0], ndp), lax.rem(me + n - shift[1], n)

    def remote(src, dst, send, recv, to):
        return pltpu.make_async_remote_copy(
            src_ref=src, dst_ref=dst, send_sem=send, recv_sem=recv, device_id=to, device_id_type=MESH
        )

    loads = [
        pltpu.make_async_copy(src.at[0], dst, load_sem.at[i])
        for i, (src, dst) in enumerate(((q_hbm, q_s), (do_hbm, do_s), (o_hbm, o_s)))
    ]
    home = dp * n + me
    loads.append(
        pltpu.make_async_copy(
            layer_hbm.at[0, :, pl.ds(pl.multiple_of(home * feats, LANES), feats)], a_s.at[home], load_sem.at[3]
        )
    )

    barrier = pltpu.get_barrier_semaphore()
    x_mates = [lax.rem(chip + k, xs) * CORES + core for k in range(1, xs)]
    mates = x_mates + [chip * CORES + (1 - core)]
    for shift in others:
        to = peer(shift)
        pl.semaphore_signal(barrier, inc=1, device_id=(to[0], to[1], tp), device_id_type=MESH)
    for mate in mates:
        pl.semaphore_signal(barrier, inc=1, device_id=(dp, me, mate), device_id_type=MESH)

    own_copies = []
    for half in range(2):
        for which, (hbm, buf) in enumerate(((k_hbm, kbuf), (v_hbm, vbuf))):
            own_copies.append(
                pltpu.make_async_copy(
                    hbm.at[0, pl.ds(half * block, block)], buf.at[half, REACH - 1], own_sem.at[half, which]
                )
            )
    for copy in own_copies + loads[:3]:
        copy.start()
    pl.semaphore_wait(barrier, len(others) + len(mates))

    def kv_pair(half, to_half, step, to):
        return [
            remote(
                hbm.at[0, pl.ds(half * block, block)],
                buf.at[to_half, REACH - 1 - step],
                kv_send.at[half, step - 1, which],
                kv_recv.at[to_half, step - 1, which],
                (dp, to, tp),
            )
            for which, (hbm, buf) in enumerate(((k_hbm, kbuf), (v_hbm, vbuf)))
        ]

    def each_kv(half, step):
        target = blocks[half] + step
        to, to_half = place_of(target, n)
        inside = target <= 2 * n - 1
        return kv_pair(half, to_half, step, to), inside & (to != me), inside & (to == me)

    for step in range(1, REACH):
        for half in range(2):
            pair, away, here = each_kv(half, step)

            @pl.when(away)
            def _():
                for copy in pair:
                    copy.start()

            if half == 0:

                @pl.when(here)
                def _():
                    for which, (hbm, buf) in enumerate(((k_hbm, kbuf), (v_hbm, vbuf))):
                        copy = pltpu.make_async_copy(
                            hbm.at[0, pl.ds(0, block)], buf.at[1, REACH - 1 - step], own_sem.at[2, which]
                        )
                        copy.start()
                        copy.wait()

    def a_copy(shift, slot):
        to = peer(shift)
        index = to[0] * n + to[1]
        return remote(
            layer_hbm.at[0, pl.ds(own_row, strip), pl.ds(pl.multiple_of(index * feats, LANES), feats)],
            a_s.at[home, pl.ds(own_row, strip)],
            a_send.at[slot],
            a_recv.at[slot],
            (to[0], to[1], tp),
        )

    a_copies = [a_copy(shift, slot) for slot, shift in enumerate(others)]
    for copy in a_copies:
        copy.start()
    loads[3].start()

    lanes = lax.broadcasted_iota(jnp.int32, (1, LANES), 1)
    low = lanes < block
    lse_s[0] = lse_ref[0]
    lse_s[1] = pltpu.roll(lse_ref[0], block, 1)
    docs = jnp.broadcast_to(doc_ref[...].astype(F32), (8, doc_ref.shape[1]))
    seq = doc_ref.shape[1]
    key_index = lax.broadcasted_iota(jnp.int32, (span, 2 * LANES), 0)
    query_index = span - block + lax.rem(lax.broadcasted_iota(jnp.int32, (span, 2 * LANES), 1), block)
    for half in range(2):
        start = (blocks[half] - (REACH - 1)) * block
        rolled = pltpu.roll(docs, lax.rem(2 * seq - start, seq), 1)[:1]
        key_row = rolled[:, :span]
        tail = rolled[:, span - LANES : span]
        query_row = jnp.where(low, pltpu.roll(jnp.broadcast_to(tail, (8, LANES)), block, 1)[:1], tail)
        key_docs = jnp.broadcast_to(key_row, (2 * LANES, span)).T
        query_docs = jnp.concatenate([query_row, query_row], axis=1)
        live = (key_index <= query_index) & (key_index + start >= 0) & (key_docs == query_docs)
        bias_s[half] = jnp.where(live, 0.0, -1e30)
        for step in range(1, REACH):

            @pl.when(blocks[half] - step < 0)
            def _():
                kbuf[half, REACH - 1 - step] = jnp.zeros((block, width), BF16)
                vbuf[half, REACH - 1 - step] = jnp.zeros((block, width), BF16)

    for copy in loads[:3] + own_copies:
        copy.wait()

    ones = jnp.ones((8, 2 * HD), BF16)

    def grad_copy(half, step):
        key_block = blocks[half] - step
        to, to_half = place_of(key_block, n)
        copy = remote(
            send_s.at[half, step - 1],
            recv_s.at[to_half, step - 1],
            g_send.at[half, step - 1],
            g_recv.at[to_half, step - 1],
            (dp, to, tp),
        )
        return copy, (key_block >= 0) & (to != me)

    for half in range(2):
        for step in range(1, REACH):
            key_block = blocks[half] - step
            holder, _ = place_of(key_block, n)

            @pl.when((key_block >= 0) & (holder != me))
            def _():
                for which, buf in enumerate((kbuf, vbuf)):
                    slot = buf.at[half, REACH - 1 - step]
                    remote(slot, slot, kv_send.at[half, step - 1, which], kv_recv.at[half, step - 1, which], (dp, holder, tp)).wait_recv()

        def group_step(g, carry):
            columns = pl.ds(pl.multiple_of(g * HD, HD), HD)
            keys = kbuf[half, :, :, columns].reshape(span, HD)
            values = vbuf[half, :, :, columns].reshape(span, HD)
            grad_key = jnp.zeros((span, HD), F32)
            grad_value = jnp.zeros((span, HD), F32)
            for part in range(per_group // stack):
                first = g * per_group + part * stack

                def stacked(ref):
                    return jnp.concatenate(
                        [
                            ref[half * block : (half + 1) * block, pl.ds(pl.multiple_of((first + j) * HD, HD), HD)]
                            for j in range(stack)
                        ],
                        axis=0,
                    )

                queries, grads, outs = stacked(q_s), stacked(do_s), stacked(o_s)
                product = grads.astype(F32) * outs.astype(F32)
                upper = product.astype(BF16)
                lower = (product - upper.astype(F32)).astype(BF16)
                delta = contract(ones, jnp.concatenate([upper, lower], axis=1), ((1,), (1,)))[:1]
                lse = jnp.concatenate(
                    [
                        jnp.where(
                            low, lse_s[half, pl.ds(first + j, 1), :], lse_s[1 - half, pl.ds(first + j + 1, 1), :]
                        )
                        for j in range(0, stack, 2)
                    ],
                    axis=1,
                )
                scores = contract(keys, queries, ((1,), (1,)))
                probs = jnp.exp(scores * scale - lse + bias_s[half])
                grad_probs = contract(values, grads, ((1,), (1,)))
                grad_scores = (probs * (grad_probs - delta)).astype(BF16)
                grad_value += contract(probs.astype(BF16), grads, ((1,), (0,)))
                grad_key += contract(grad_scores, queries, ((1,), (0,)))
                grad_query = (contract(grad_scores, keys, ((0,), (0,))) * scale).astype(BF16)
                for j in range(stack):
                    dq_s[half * block : (half + 1) * block, pl.ds(pl.multiple_of((first + j) * HD, HD), HD)] = grad_query[
                        j * block : (j + 1) * block
                    ]
            dkv_s[:, columns] = grad_key * scale
            dkv_s[:, pl.ds(pl.multiple_of(width + g * HD, HD), HD)] = grad_value
            return carry

        lax.fori_loop(0, groups, group_step, 0)
        acc_s[half] = dkv_s[span - block :]
        for step in range(1, REACH):
            at = (REACH - 1 - step) * block
            send_s[half, step - 1] = dkv_s[at : at + block].astype(BF16)
        for step in range(1, REACH):
            copy, away = grad_copy(half, step)

            @pl.when(away)
            def _():
                copy.start()

    dq_out = pltpu.make_async_copy(dq_s, dq_hbm.at[0], out_sem.at[0])
    dq_out.start()

    x_copies, c_copies = [], []
    for slot, shift in enumerate(others):
        a_copies[slot].wait_recv()
        from_dp, from_ctx = source(shift)
        index = from_dp * n + from_ctx
        piece = a_s.at[index, pl.ds(own_row, strip)]
        for k, mate in enumerate(x_mates):
            copy = remote(piece, piece, x_send.at[slot, k], x_recv.at[slot, k], (dp, me, mate))
            copy.start()
            x_copies.append(copy)

    for half in range(2):
        for step in range(1, REACH):
            target = blocks[half] + step
            to, _ = place_of(target, n)

            @pl.when((target <= 2 * n - 1) & (to != me))
            def _():
                slot = recv_s.at[half, step - 1]
                remote(slot, slot, g_send.at[half, step - 1], g_recv.at[half, step - 1], (dp, to, tp)).wait_recv()
                acc_s[half] += recv_s[half, step - 1].astype(F32)

            if half == 0:

                @pl.when(to == me)
                def _():
                    acc_s[0] += send_s[1, step - 1].astype(F32)

    for half in range(2):
        dk_ref[0, half * block : (half + 1) * block] = acc_s[half, :, :width].astype(BF16)
        grad_value = acc_s[half, :, width:].astype(BF16)
        dv_ref[0, half * block : (half + 1) * block] = grad_value
        vg_s[home, half * block : (half + 1) * block] = grad_value

    def vg_copy(index, slot, to):
        return remote(vg_s.at[index], vg_s.at[index], vg_send.at[slot], vg_recv.at[slot], (to[0], to[1], tp))

    vg_copies = {}
    for shift in others:
        if 0 in shift:
            vg_copies[shift] = vg_copy(home, shift[0] * n + shift[1], peer(shift))
            vg_copies[shift].start()

    for slot, shift in enumerate(others):
        from_dp, from_ctx = source(shift)
        index = from_dp * n + from_ctx
        for k in range(xs - 1):
            x_copies[slot * (xs - 1) + k].wait_recv()
        piece = a_s.at[index, pl.ds(core_row, xs * strip)]
        copy = remote(piece, piece, c_send.at[slot], c_recv.at[slot], (dp, me, mates[-1]))
        copy.start()
        c_copies.append(copy)

    for b in range(1, n):
        vg_copies[(0, b)].wait_recv()
        from_ctx = lax.rem(me + n - b, n)
        for a in range(1, ndp):
            copy = vg_copy(dp * n + from_ctx, a * n + b, (lax.rem(dp + a, ndp), me))
            copy.start()
            vg_copies[(a, b)] = copy

    loads[3].wait()
    for slot in range(len(others)):
        c_copies[slot].wait_recv()

    def flip(s, carry):
        at_s[:, pl.ds(pl.multiple_of(s * rows, LANES), rows)] = a_s[s].T
        return carry

    lax.fori_loop(0, ndp * n, flip, 0)
    for shift in others:
        if shift[0] != 0:
            vg_copies[shift].wait_recv()
    token_scale = (ndp * seq) ** (-0.5)
    grads_all = vg_s[...].reshape(ndp * n * rows, width)
    tile = 2 * LANES

    def tile_copy(t):
        at = pl.ds(pl.multiple_of(t * tile, tile), tile)
        return pltpu.make_async_copy(w_s.at[at], w_hbm.at[at], out_sem.at[1 + t])

    for t in range(feats // tile):
        w_s[t * tile : (t + 1) * tile] = (
            contract(at_s[t * tile : (t + 1) * tile], grads_all, ((1,), (0,))) * token_scale
        )
        tile_copy(t).start()

    dq_out.wait()
    for t in range(feats // tile):
        tile_copy(t).wait()
    for copy in a_copies + x_copies + c_copies + list(vg_copies.values()):
        copy.wait_send()
    for half in range(2):
        for step in range(1, REACH):
            pair, away, _ = each_kv(half, step)

            @pl.when(away)
            def _():
                for copy in pair:
                    copy.wait_send()

            copy, away = grad_copy(half, step)

            @pl.when(away)
            def _():
                copy.wait_send()


def fused_body(sizes, layer_input, queries, key_heads, value_heads, attn_out, out_grad, log_sums, doc_ids):
    ndp, n, ntp = sizes
    rows, head_width = queries.shape[1:]
    width = key_heads.shape[2]
    block = rows // 2
    span = REACH * block
    peers = ndp * n
    feats = layer_input.shape[2] // peers
    xs = ntp // CORES
    hops = REACH - 1
    dma = pltpu.SemaphoreType.DMA
    hbm = pl.BlockSpec(memory_space=pl.ANY)
    vmem = pl.BlockSpec(memory_space=pltpu.VMEM)
    return pl.pallas_call(
        functools.partial(fused_kernel, sizes),
        out_shape=(
            jax.ShapeDtypeStruct(queries.shape, BF16),
            jax.ShapeDtypeStruct(key_heads.shape, BF16),
            jax.ShapeDtypeStruct(key_heads.shape, BF16),
            jax.ShapeDtypeStruct((feats, width), F32),
        ),
        in_specs=[hbm] * 6 + [vmem] * 2,
        out_specs=(hbm, vmem, vmem, hbm),
        scratch_shapes=[
            pltpu.VMEM((rows, head_width), BF16),
            pltpu.VMEM((rows, head_width), BF16),
            pltpu.VMEM((rows, head_width), BF16),
            pltpu.VMEM((rows, head_width), BF16),
            pltpu.VMEM((2, REACH, block, width), BF16),
            pltpu.VMEM((2, REACH, block, width), BF16),
            pltpu.VMEM((2, span, 2 * LANES), F32),
            pltpu.VMEM((2, head_width // HD, rows), F32),
            pltpu.VMEM((span, 2 * width), F32),
            pltpu.VMEM((2, block, 2 * width), F32),
            pltpu.VMEM((2, hops, block, 2 * width), BF16),
            pltpu.VMEM((2, hops, block, 2 * width), BF16),
            pltpu.VMEM((peers, rows, feats), BF16),
            pltpu.VMEM((feats, peers * rows), BF16),
            pltpu.VMEM((peers, rows, width), BF16),
            pltpu.VMEM((feats, width), F32),
            dma((4,)),
            dma((3, 2)),
            dma((2, hops, 2)),
            dma((2, hops, 2)),
            dma((2, hops)),
            dma((2, hops)),
            dma((peers - 1,)),
            dma((peers - 1,)),
            dma((peers - 1, xs - 1)),
            dma((peers - 1, xs - 1)),
            dma((peers - 1,)),
            dma((peers - 1,)),
            dma((peers,)),
            dma((peers,)),
            dma((1 + feats // (2 * LANES),)),
        ],
        compiler_params=pltpu.CompilerParams(
            collective_id=0, has_side_effects=True, vmem_limit_bytes=48 * 1024 * 1024
        ),
    )(layer_input, queries, key_heads, value_heads, attn_out, out_grad, log_sums, doc_ids)


def with_halo(cells, sides, width):
    for axis, dim in sides:
        count = lax.axis_size(axis)
        ends = count - 1
        head = lax.slice_in_dim(cells, 0, width, axis=dim)
        tail = lax.slice_in_dim(cells, cells.shape[dim] - width, cells.shape[dim], axis=dim)
        cells = jnp.concatenate(
            [
                lax.ppermute(tail, axis, [(i, (i + 1) % count) for i in range(ends)]),
                cells,
                lax.ppermute(head, axis, [((i + 1) % count, i) for i in range(ends)]),
            ],
            axis=dim,
        )
    return cells


def tile_terms(query_rows, grad_rows, lse_rows, row_delta, key_value, live_mask):
    groups = query_rows.shape[1]
    score_scale = HD ** (-0.5)
    key_rows = key_value[:, : groups * HD].reshape(-1, groups, HD)
    value_rows = key_value[:, groups * HD :].reshape(-1, groups, HD)
    scores = (
        jnp.einsum("qgrd,kgd->grqk", query_rows, key_rows, preferred_element_type=jnp.float32)
        * score_scale
    )
    soft_probs = jnp.where(live_mask, jnp.exp(scores - lse_rows[..., None]), 0.0)
    grad_value = jnp.einsum(
        "grqk,qgrd->kgd",
        soft_probs.astype(jnp.bfloat16),
        grad_rows,
        preferred_element_type=jnp.float32,
    )
    grad_probs = jnp.einsum(
        "qgrd,kgd->grqk", grad_rows, value_rows, preferred_element_type=jnp.float32
    )
    grad_scores = (soft_probs * (grad_probs - row_delta[..., None])).astype(jnp.bfloat16)
    grad_query = (
        jnp.einsum("grqk,kgd->qgrd", grad_scores, key_rows, preferred_element_type=jnp.float32)
        * score_scale
    )
    grad_key = (
        jnp.einsum("grqk,qgrd->kgd", grad_scores, query_rows, preferred_element_type=jnp.float32)
        * score_scale
    )
    key_count = key_value.shape[0]
    joined = jnp.concatenate(
        [grad_key.reshape(key_count, groups * HD), grad_value.reshape(key_count, groups * HD)],
        axis=1,
    )
    return (grad_query, joined)


def block_terms(
    reach_step,
    query_block,
    key_block,
    doc_seq,
    block_rows,
    query_rows,
    grad_rows,
    lse_rows,
    row_delta,
    key_value,
):
    query_doc = lax.dynamic_slice_in_dim(doc_seq, query_block * block_rows, block_rows)
    key_doc = lax.dynamic_slice_in_dim(doc_seq, jnp.maximum(key_block, 0) * block_rows, block_rows)
    offsets = jnp.arange(block_rows, dtype=jnp.int32)
    query_pos = query_block * block_rows + offsets
    key_pos = key_block * block_rows + offsets
    live_mask = (
        (key_pos[None, :] <= query_pos[:, None])
        & (key_doc[None, :] == query_doc[:, None])
        & (key_block >= 0)
    )
    operands = (query_rows, grad_rows, lse_rows, row_delta, key_value, live_mask)
    if reach_step == 0:
        return tile_terms(*operands)

    def compute(packed):
        return tile_terms(*packed)

    def skipped(packed):
        return (jnp.zeros(packed[0].shape, jnp.float32), jnp.zeros(packed[4].shape, jnp.float32))

    live_tile = (key_block >= 0) & (key_doc[block_rows - 1] == query_doc[0])
    return lax.cond(live_tile, compute, skipped, operands)


def body(layer_input, queries, key_heads, value_heads, attn_out, out_grad, log_sums, doc_ids):
    ctx_index = lax.axis_index("ctx")
    ctx_count = lax.axis_size("ctx")
    block_rows = queries.shape[1] // 2
    kv_width = key_heads.shape[2]
    groups = kv_width // HD
    head_count = queries.shape[2] // HD
    per_group = head_count // groups
    query_rows = queries[0].reshape(2, block_rows, groups, per_group, HD)
    grad_rows = out_grad[0].reshape(2, block_rows, groups, per_group, HD)
    out_rows = attn_out[0].reshape(2, block_rows, groups, per_group, HD)
    row_delta = jnp.sum(
        grad_rows.astype(jnp.float32) * out_rows.astype(jnp.float32), axis=-1
    ).transpose(0, 2, 3, 1)
    lse_rows = log_sums[0].reshape(groups, per_group, 2, block_rows).transpose(2, 0, 1, 3)
    doc_seq = doc_ids[0]
    own_blocks = (ctx_index, 2 * ctx_count - 1 - ctx_index)
    key_value = jnp.concatenate([key_heads[0], value_heads[0]], axis=1)
    current = (key_value[:block_rows], key_value[block_rows:])
    last_device = ctx_index == ctx_count - 1
    query_accum = [
        jnp.zeros(query_rows.shape[1:], jnp.float32),
        jnp.zeros(query_rows.shape[1:], jnp.float32),
    ]
    pieces = []
    for reach_step in range(REACH):
        if reach_step > 0:
            stacked = jnp.concatenate([current[1], current[0]], axis=0)
            padded = with_halo(stacked, (("ctx", 0),), block_rows)
            current = (
                padded[:block_rows],
                jnp.where(last_device, current[0], padded[3 * block_rows :]),
            )
        grad_terms = []
        for which_half in range(2):
            query_block = own_blocks[which_half]
            grad_query, joined = block_terms(
                reach_step,
                query_block,
                query_block - reach_step,
                doc_seq,
                block_rows,
                query_rows[which_half],
                grad_rows[which_half],
                lse_rows[which_half],
                row_delta[which_half],
                current[which_half],
            )
            query_accum[which_half] = query_accum[which_half] + grad_query
            grad_terms.append(joined)
        pieces.append(grad_terms)
    accum_first, accum_second = pieces[REACH - 1]
    for reach_step in range(REACH - 1, 0, -1):
        stacked = jnp.concatenate([accum_first, accum_second], axis=0)
        padded = with_halo(stacked, (("ctx", 0),), block_rows)
        accum_first, accum_second = (
            jnp.where(last_device, accum_second, padded[3 * block_rows :])
            + pieces[reach_step - 1][0],
            padded[:block_rows] + pieces[reach_step - 1][1],
        )
    kv_grad = jnp.concatenate([accum_first, accum_second], axis=0)
    key_grad = kv_grad[:, :kv_width].astype(jnp.bfloat16)
    value_grad = kv_grad[:, kv_width:].astype(jnp.bfloat16)
    query_grad = (
        jnp.concatenate(query_accum, axis=0)
        .reshape(1, 2 * block_rows, head_count * HD)
        .astype(jnp.bfloat16)
    )
    tokens = layer_input[0]
    weight_scale = (lax.axis_size("dp") * doc_seq.shape[0]) ** (-0.5)
    weight_grad = lax.psum_scatter(
        jnp.einsum("td,tc->dc", tokens, value_grad, preferred_element_type=jnp.float32)
        * weight_scale,
        ("dp", "ctx"),
        scatter_dimension=0,
        tiled=True,
    )
    return (query_grad, key_grad[None], value_grad[None], weight_grad)


def fits(mesh, queries_shape, layer_shape, seq):
    ndp, n, ntp = (mesh.shape[axis] for axis in ("dp", "ctx", "tp"))
    feats = layer_shape[2] // (ndp * n)
    rows = queries_shape[1] // n
    return (
        ndp * n <= 16
        and n >= REACH
        and ntp > CORES
        and ntp % CORES == 0
        and feats % (2 * LANES) == 0
        and rows == LANES
        and rows % (16 * ntp) == 0
        and seq % LANES == 0
    )


def solution(mesh):
    sizes = tuple(mesh.shape[axis] for axis in ("dp", "ctx", "tp"))
    in_specs = (
        P("dp", "ctx", None),
        P("dp", "ctx", "tp"),
        P("dp", "ctx", "tp"),
        P("dp", "ctx", "tp"),
        P("dp", "ctx", "tp"),
        P("dp", "ctx", "tp"),
        P("dp", "tp", "ctx"),
        P("dp", None),
    )
    out_specs = (
        P("dp", "ctx", "tp"),
        P("dp", "ctx", "tp"),
        P("dp", "ctx", "tp"),
        P(("dp", "ctx"), "tp"),
    )

    def run(layer_input, queries, *rest):
        fused = fits(mesh, queries.shape, layer_input.shape, rest[-1].shape[1])
        chosen = functools.partial(fused_body, sizes) if fused else body
        return jax.shard_map(chosen, mesh=mesh, in_specs=in_specs, out_specs=out_specs, check_vma=False)(
            layer_input, queries, *rest
        )

    return run
```

profile of v0, /device:TPU:0, one launch (start us, length us, event | category | flops | bytes accessed | tf_op | source)
XLA Modules:
  0.0 55.7 jit_solution(5866878788494836820)
XLA Ops:
  0.6 0.0 copy-start
  0.6 1.2 %copy-done = bf16[1,128,4096]{2,1,0:T(8,128)(2,1)S(1)} copy-done((bf16[1,128,4096]{2,1,0:T(8,128)(2,1)S(1)}, bf16[1,128,4096]{2,1,0:T(8,128)(2,1)}, u32[]{:S(2)}) %copy-start) | copy-done | bytes 1048600
  1.9 0.0 copy-start.1
  1.9 1.2 %copy-done.1 = bf16[1,128,4096]{2,1,0:T(8,128)(2,1)S(1)} copy-done((bf16[1,128,4096]{2,1,0:T(8,128)(2,1)S(1)}, bf16[1,128,4096]{2,1,0:T(8,128)(2,1)}, u32[]{:S(2)}) %copy-start.1) | copy-done | bytes 1048600
  3.1 0.0 copy-start.2
  3.1 1.2 %copy-done.2 = bf16[1,128,4096]{2,1,0:T(8,128)(2,1)S(1)} copy-done((bf16[1,128,4096]{2,1,0:T(8,128)(2,1)S(1)}, bf16[1,128,4096]{2,1,0:T(8,128)(2,1)}, u32[]{:S(2)}) %copy-start.2) | copy-done | bytes 1048600
  4.3 0.0 copy-start.3
  4.3 0.8 %copy-done.3 = bf16[1,128,256]{2,1,0:T(8,128)(2,1)S(1)} copy-done((bf16[1,128,256]{2,1,0:T(8,128)(2,1)S(1)}, bf16[1,128,256]{2,1,0:T(8,128)(2,1)}, u32[]{:S(2)}) %copy-start.3) | copy-done | bytes 65560
  5.2 0.0 copy-start.4
  5.2 0.8 %copy-done.4 = bf16[1,128,256]{2,1,0:T(8,128)(2,1)S(1)} copy-done((bf16[1,128,256]{2,1,0:T(8,128)(2,1)S(1)}, bf16[1,128,256]{2,1,0:T(8,128)(2,1)}, u32[]{:S(2)}) %copy-start.4) | copy-done | bytes 65560
  6.0 0.0 copy-start.5
  6.0 0.7 %copy-done.5 = f32[1,32,128]{2,1,0:T(8,128)S(1)} copy-done((f32[1,32,128]{2,1,0:T(8,128)S(1)}, f32[1,32,128]{2,1,0:T(8,128)}, u32[]{:S(2)}) %copy-start.5) | copy-done | bytes 16408
  6.7 0.0 copy-start.6
  6.7 0.7 %copy-done.6 = s32[1,512]{1,0:T(1,128)S(1)} copy-done((s32[1,512]{1,0:T(1,128)S(1)}, s32[1,512]{1,0:T(1,128)}, u32[]{:S(2)}) %copy-start.6) | copy-done | bytes 2072
  7.4 45.1 %shard_map.111 = (bf16[1,128,4096]{2,1,0:T(8,128)(2,1)S(1)}, bf16[1,128,256]{2,1,0:T(8,128)(2,1)S(1)}, bf16[1,128,256]{2,1,0:T(8,128)(2,1)S(1)}, f32[1024,256]{1,0:T(8,128)S(1)}) custom-call(bf16[1,128,8192]{2,1,0:T(8,128)(2,1)} %layer_hbm.1, bf16[1,128,4096]{2,1,0:T(8,128)(2,1)S(1)} %copy-done, bf16[1,128,256]{2,1,0:T(8,128)(2,1)S(1)} %copy-done.3, ...), custom_call_target="tpu_custom_call" | custom-call | tf_op jit(solution)/shard_map/pallas_call | solution.py:426
  52.5 1.0 %copy.16 = bf16[1,128,4096]{2,1,0:T(8,128)(2,1)} copy(bf16[1,128,4096]{2,1,0:T(8,128)(2,1)S(1)} %get-tuple-element.8) | data formatting | bytes 2097152
  53.5 0.6 %copy.17 = bf16[1,128,256]{2,1,0:T(8,128)(2,1)} copy(bf16[1,128,256]{2,1,0:T(8,128)(2,1)S(1)} %get-tuple-element.9) | data formatting | bytes 131072
  54.1 0.6 %copy.18 = bf16[1,128,256]{2,1,0:T(8,128)(2,1)} copy(bf16[1,128,256]{2,1,0:T(8,128)(2,1)S(1)} %get-tuple-element.10) | data formatting | bytes 131072
  54.7 1.0 %copy.19 = f32[1024,256]{1,0:T(8,128)} copy(f32[1024,256]{1,0:T(8,128)S(1)} %get-tuple-element.11) | data formatting | bytes 2097152
Async XLA Ops:
  0.6 1.2 %copy-start = (bf16[1,128,4096]{2,1,0:T(8,128)(2,1)S(1)}, bf16[1,128,4096]{2,1,0:T(8,128)(2,1)}, u32[]{:S(2)}) copy-start(bf16[1,128,4096]{2,1,0:T(8,128)(2,1)} %q_hbm.1) | copy-start | bytes 3145732
  1.9 1.2 %copy-start.1 = (bf16[1,128,4096]{2,1,0:T(8,128)(2,1)S(1)}, bf16[1,128,4096]{2,1,0:T(8,128)(2,1)}, u32[]{:S(2)}) copy-start(bf16[1,128,4096]{2,1,0:T(8,128)(2,1)} %o_hbm.1) | copy-start | bytes 3145732
  3.1 1.2 %copy-start.2 = (bf16[1,128,4096]{2,1,0:T(8,128)(2,1)S(1)}, bf16[1,128,4096]{2,1,0:T(8,128)(2,1)}, u32[]{:S(2)}) copy-start(bf16[1,128,4096]{2,1,0:T(8,128)(2,1)} %do_hbm.1) | copy-start | bytes 3145732
  4.3 0.8 %copy-start.3 = (bf16[1,128,256]{2,1,0:T(8,128)(2,1)S(1)}, bf16[1,128,256]{2,1,0:T(8,128)(2,1)}, u32[]{:S(2)}) copy-start(bf16[1,128,256]{2,1,0:T(8,128)(2,1)} %k_hbm.1) | copy-start | bytes 196612
  5.2 0.8 %copy-start.4 = (bf16[1,128,256]{2,1,0:T(8,128)(2,1)S(1)}, bf16[1,128,256]{2,1,0:T(8,128)(2,1)}, u32[]{:S(2)}) copy-start(bf16[1,128,256]{2,1,0:T(8,128)(2,1)} %v_hbm.1) | copy-start | bytes 196612
  6.0 0.7 %copy-start.5 = (f32[1,32,128]{2,1,0:T(8,128)S(1)}, f32[1,32,128]{2,1,0:T(8,128)}, u32[]{:S(2)}) copy-start(f32[1,32,128]{2,1,0:T(8,128)} %lse_ref.1) | copy-start | bytes 49156
  6.7 0.7 %copy-start.6 = (s32[1,512]{1,0:T(1,128)S(1)}, s32[1,512]{1,0:T(1,128)}, u32[]{:S(2)}) copy-start(s32[1,512]{1,0:T(1,128)} %doc_ref.1) | copy-start | bytes 6148
where the time goes:
time: 56.1 us; the launch traced here: 55.7 us
  Pallas kernels  45.1 us (80%)
  local copies, waits for them, and re-layouts  9.94 us (18%)
  between operations  0.66 us (1%)
    pallas_call x1, Pallas kernels, fused_body(): pl.pallas_call(functools.partial(fused_kernel, sizes), out_shape=(jax.Sha...  45.1 us
    unnamed x18, local copies, waits for them, and re-layouts  9.94 us

commit v1 on v0

--- a/solution.py
+++ b/solution.py
@@ -10,6 +10,7 @@
 HD = 128
 LANES = 128
 CORES = 2
+EARLY = 7
 MESH = pl.DeviceIdType.MESH
 F32 = jnp.float32
 BF16 = jnp.bfloat16
@@ -31,28 +32,29 @@
     v_hbm,
     o_hbm,
     do_hbm,
-    lse_ref,
-    doc_ref,
-    dq_hbm,
+    lse_hbm,
+    doc_hbm,
+    dq_ref,
     dk_ref,
     dv_ref,
-    w_hbm,
+    w_s,
     q_s,
     o_s,
     do_s,
-    dq_s,
+    lse_in,
+    doc_ref,
     kbuf,
     vbuf,
     bias_s,
     lse_s,
     dkv_s,
     acc_s,
+    held_s,
     send_s,
     recv_s,
     a_s,
     at_s,
     vg_s,
-    w_s,
     load_sem,
     own_sem,
     kv_send,
@@ -67,7 +69,6 @@
     c_recv,
     vg_send,
     vg_recv,
-    out_sem,
 ):
     ndp, n, ntp = sizes
     dp, me, tp = lax.axis_index("dp"), lax.axis_index("ctx"), lax.axis_index("tp")
@@ -105,6 +106,10 @@
         pltpu.make_async_copy(src.at[0], dst, load_sem.at[i])
         for i, (src, dst) in enumerate(((q_hbm, q_s), (do_hbm, do_s), (o_hbm, o_s)))
     ]
+    small = [
+        pltpu.make_async_copy(lse_hbm.at[0], lse_in, load_sem.at[4]),
+        pltpu.make_async_copy(doc_hbm, doc_ref, load_sem.at[5]),
+    ]
     home = dp * n + me
     loads.append(
         pltpu.make_async_copy(
@@ -129,7 +134,7 @@
                     hbm.at[0, pl.ds(half * block, block)], buf.at[half, REACH - 1], own_sem.at[half, which]
                 )
             )
-    for copy in own_copies + loads[:3]:
+    for copy in small + own_copies + loads[:3]:
         copy.start()
     pl.semaphore_wait(barrier, len(others) + len(mates))
 
@@ -145,10 +150,15 @@
             for which, (hbm, buf) in enumerate(((k_hbm, kbuf), (v_hbm, vbuf)))
         ]
 
+    def here_copy(hbm, buf, step, which):
+        return pltpu.make_async_copy(
+            hbm.at[0, pl.ds(0, block)], buf.at[1, REACH - 1 - step], own_sem.at[1 + step, which]
+        )
+
     def each_kv(half, step):
         target = blocks[half] + step
         to, to_half = place_of(target, n)
-        inside = target <= 2 * n - 1
+        inside = (target <= 2 * n - 1) & (target != n)
         return kv_pair(half, to_half, step, to), inside & (to != me), inside & (to == me)
 
     for step in range(1, REACH):
@@ -165,11 +175,7 @@
                 @pl.when(here)
                 def _():
                     for which, (hbm, buf) in enumerate(((k_hbm, kbuf), (v_hbm, vbuf))):
-                        copy = pltpu.make_async_copy(
-                            hbm.at[0, pl.ds(0, block)], buf.at[1, REACH - 1 - step], own_sem.at[2, which]
-                        )
-                        copy.start()
-                        copy.wait()
+                        here_copy(hbm, buf, step, which).start()
 
     def a_copy(shift, slot):
         to = peer(shift)
@@ -183,14 +189,16 @@
         )
 
     a_copies = [a_copy(shift, slot) for slot, shift in enumerate(others)]
-    for copy in a_copies:
+    for copy in a_copies[:EARLY]:
         copy.start()
     loads[3].start()
 
+    for copy in small:
+        copy.wait()
     lanes = lax.broadcasted_iota(jnp.int32, (1, LANES), 1)
     low = lanes < block
-    lse_s[0] = lse_ref[0]
-    lse_s[1] = pltpu.roll(lse_ref[0], block, 1)
+    lse_s[0] = lse_in[...]
+    lse_s[1] = pltpu.roll(lse_in[...], block, 1)
     docs = jnp.broadcast_to(doc_ref[...].astype(F32), (8, doc_ref.shape[1]))
     seq = doc_ref.shape[1]
     key_index = lax.broadcasted_iota(jnp.int32, (span, 2 * LANES), 0)
@@ -214,6 +222,15 @@
 
     for copy in loads[:3] + own_copies:
         copy.wait()
+    last = me == n - 1
+    for step in range(1, REACH):
+        here = each_kv(0, step)[2]
+
+        @pl.when(here)
+        def _():
+            for which, (hbm, buf) in enumerate(((k_hbm, kbuf), (v_hbm, vbuf))):
+                here_copy(hbm, buf, step, which).wait()
+
 
     ones = jnp.ones((8, 2 * HD), BF16)
 
@@ -227,18 +244,29 @@
             g_recv.at[to_half, step - 1],
             (dp, to, tp),
         )
-        return copy, (key_block >= 0) & (to != me)
+        away = (key_block >= 0) & (to != me)
+        if half == 0 and step < REACH - 1:
+            away &= key_block + step != n - 1
+        return copy, away
 
     for half in range(2):
         for step in range(1, REACH):
             key_block = blocks[half] - step
             holder, _ = place_of(key_block, n)
 
-            @pl.when((key_block >= 0) & (holder != me))
+            @pl.when((key_block >= 0) & (holder != me) & (blocks[half] != n))
             def _():
                 for which, buf in enumerate((kbuf, vbuf)):
                     slot = buf.at[half, REACH - 1 - step]
                     remote(slot, slot, kv_send.at[half, step - 1, which], kv_recv.at[half, step - 1, which], (dp, holder, tp)).wait_recv()
+
+        if half == 1:
+
+            @pl.when(last)
+            def _():
+                for buf in (kbuf, vbuf):
+                    for step in range(1, REACH):
+                        buf[1, REACH - 1 - step] = buf[0, REACH - step]
 
         def group_step(g, carry):
             columns = pl.ds(pl.multiple_of(g * HD, HD), HD)
@@ -280,7 +308,7 @@
                 grad_key += contract(grad_scores, queries, ((1,), (0,)))
                 grad_query = (contract(grad_scores, keys, ((0,), (0,))) * scale).astype(BF16)
                 for j in range(stack):
-                    dq_s[half * block : (half + 1) * block, pl.ds(pl.multiple_of((first + j) * HD, HD), HD)] = grad_query[
+                    dq_ref[0, half * block : (half + 1) * block, pl.ds(pl.multiple_of((first + j) * HD, HD), HD)] = grad_query[
                         j * block : (j + 1) * block
                     ]
             dkv_s[:, columns] = grad_key * scale
@@ -292,6 +320,14 @@
         for step in range(1, REACH):
             at = (REACH - 1 - step) * block
             send_s[half, step - 1] = dkv_s[at : at + block].astype(BF16)
+            if half == 0 and step < REACH - 1:
+                held_s[step - 1] = dkv_s[at : at + block]
+            if half == 1 and step > 1:
+
+                @pl.when(last)
+                def _():
+                    send_s[1, step - 1] = (dkv_s[at : at + block] + held_s[step - 2]).astype(BF16)
+
         for step in range(1, REACH):
             copy, away = grad_copy(half, step)
 
@@ -299,26 +335,56 @@
             def _():
                 copy.start()
 
-    dq_out = pltpu.make_async_copy(dq_s, dq_hbm.at[0], out_sem.at[0])
-    dq_out.start()
-
-    x_copies, c_copies = [], []
-    for slot, shift in enumerate(others):
-        a_copies[slot].wait_recv()
+    for copy in a_copies[EARLY:]:
+        copy.start()
+
+    x_copies, c_copies = {}, {}
+
+    def slot_of(shift):
         from_dp, from_ctx = source(shift)
-        index = from_dp * n + from_ctx
-        piece = a_s.at[index, pl.ds(own_row, strip)]
-        for k, mate in enumerate(x_mates):
-            copy = remote(piece, piece, x_send.at[slot, k], x_recv.at[slot, k], (dp, me, mate))
-            copy.start()
-            x_copies.append(copy)
+        return from_dp * n + from_ctx
+
+    def share_with_chips(slots):
+        for slot in slots:
+            a_copies[slot].wait_recv()
+            piece = a_s.at[slot_of(others[slot]), pl.ds(own_row, strip)]
+            for k, mate in enumerate(x_mates):
+                x_copies[slot, k] = remote(piece, piece, x_send.at[slot, k], x_recv.at[slot, k], (dp, me, mate))
+                x_copies[slot, k].start()
+
+    def share_with_core(slots):
+        for slot in slots:
+            for k in range(xs - 1):
+                x_copies[slot, k].wait_recv()
+            piece = a_s.at[slot_of(others[slot]), pl.ds(core_row, xs * strip)]
+            c_copies[slot] = remote(piece, piece, c_send.at[slot], c_recv.at[slot], (dp, me, mates[-1]))
+            c_copies[slot].start()
+
+    def flip(s):
+        at_s[:, pl.ds(pl.multiple_of(s * rows, LANES), rows)] = a_s[s].T
+
+    def flip_all(slots):
+        for slot in slots:
+            c_copies[slot].wait_recv()
+        shifts = [others[slot] for slot in slots]
+        for shift in shifts:
+            flip(slot_of(shift))
+
+    early, late = range(EARLY), range(EARLY, len(others))
+    share_with_chips(early)
+    loads[3].wait()
+    flip(home)
 
     for half in range(2):
         for step in range(1, REACH):
             target = blocks[half] + step
             to, _ = place_of(target, n)
 
-            @pl.when((target <= 2 * n - 1) & (to != me))
+            arrives = (target <= 2 * n - 1) & (to != me)
+            if step < REACH - 1:
+                arrives &= target != n - 1
+
+            @pl.when(arrives)
             def _():
                 slot = recv_s.at[half, step - 1]
                 remote(slot, slot, g_send.at[half, step - 1], g_recv.at[half, step - 1], (dp, to, tp)).wait_recv()
@@ -344,34 +410,18 @@
         if 0 in shift:
             vg_copies[shift] = vg_copy(home, shift[0] * n + shift[1], peer(shift))
             vg_copies[shift].start()
-
-    for slot, shift in enumerate(others):
-        from_dp, from_ctx = source(shift)
-        index = from_dp * n + from_ctx
-        for k in range(xs - 1):
-            x_copies[slot * (xs - 1) + k].wait_recv()
-        piece = a_s.at[index, pl.ds(core_row, xs * strip)]
-        copy = remote(piece, piece, c_send.at[slot], c_recv.at[slot], (dp, me, mates[-1]))
-        copy.start()
-        c_copies.append(copy)
-
-    for b in range(1, n):
+    share_with_chips(late)
+    share_with_core(early)
+    near = sorted(range(1, n), key=lambda b: min(b, n - b))
+    share_with_core(late)
+    for b in near:
         vg_copies[(0, b)].wait_recv()
         from_ctx = lax.rem(me + n - b, n)
         for a in range(1, ndp):
-            copy = vg_copy(dp * n + from_ctx, a * n + b, (lax.rem(dp + a, ndp), me))
-            copy.start()
-            vg_copies[(a, b)] = copy
-
-    loads[3].wait()
-    for slot in range(len(others)):
-        c_copies[slot].wait_recv()
-
-    def flip(s, carry):
-        at_s[:, pl.ds(pl.multiple_of(s * rows, LANES), rows)] = a_s[s].T
-        return carry
-
-    lax.fori_loop(0, ndp * n, flip, 0)
+            vg_copies[(a, b)] = vg_copy(dp * n + from_ctx, a * n + b, (lax.rem(dp + a, ndp), me))
+            vg_copies[(a, b)].start()
+    flip_all(early)
+    flip_all(late)
     for shift in others:
         if shift[0] != 0:
             vg_copies[shift].wait_recv()
@@ -379,20 +429,12 @@
     grads_all = vg_s[...].reshape(ndp * n * rows, width)
     tile = 2 * LANES
 
-    def tile_copy(t):
-        at = pl.ds(pl.multiple_of(t * tile, tile), tile)
-        return pltpu.make_async_copy(w_s.at[at], w_hbm.at[at], out_sem.at[1 + t])
-
     for t in range(feats // tile):
         w_s[t * tile : (t + 1) * tile] = (
             contract(at_s[t * tile : (t + 1) * tile], grads_all, ((1,), (0,))) * token_scale
         )
-        tile_copy(t).start()
-
-    dq_out.wait()
-    for t in range(feats // tile):
-        tile_copy(t).wait()
-    for copy in a_copies + x_copies + c_copies + list(vg_copies.values()):
+
+    for copy in a_copies + list(x_copies.values()) + list(c_copies.values()) + list(vg_copies.values()):
         copy.wait_send()
     for half in range(2):
         for step in range(1, REACH):
@@ -408,6 +450,14 @@
             @pl.when(away)
             def _():
                 copy.wait_send()
+
+
+def store_kernel(*refs):
+    copies = [pltpu.make_async_copy(refs[i], refs[4 + i], refs[8].at[i]) for i in range(4)]
+    for copy in copies:
+        copy.start()
+    for copy in copies:
+        copy.wait()
 
 
 def fused_body(sizes, layer_input, queries, key_heads, value_heads, attn_out, out_grad, log_sums, doc_ids):
@@ -421,9 +471,9 @@
     xs = ntp // CORES
     hops = REACH - 1
     dma = pltpu.SemaphoreType.DMA
-    hbm = pl.BlockSpec(memory_space=pl.ANY)
+    hbm = pl.BlockSpec(memory_space=pltpu.HBM)
     vmem = pl.BlockSpec(memory_space=pltpu.VMEM)
-    return pl.pallas_call(
+    results = pl.pallas_call(
         functools.partial(fused_kernel, sizes),
         out_shape=(
             jax.ShapeDtypeStruct(queries.shape, BF16),
@@ -431,27 +481,28 @@
             jax.ShapeDtypeStruct(key_heads.shape, BF16),
             jax.ShapeDtypeStruct((feats, width), F32),
         ),
-        in_specs=[hbm] * 6 + [vmem] * 2,
-        out_specs=(hbm, vmem, vmem, hbm),
+        in_specs=[hbm] * 8,
+        out_specs=(vmem,) * 4,
         scratch_shapes=[
             pltpu.VMEM((rows, head_width), BF16),
             pltpu.VMEM((rows, head_width), BF16),
             pltpu.VMEM((rows, head_width), BF16),
-            pltpu.VMEM((rows, head_width), BF16),
+            pltpu.VMEM(log_sums.shape[1:], F32),
+            pltpu.VMEM(doc_ids.shape, jnp.int32),
             pltpu.VMEM((2, REACH, block, width), BF16),
             pltpu.VMEM((2, REACH, block, width), BF16),
             pltpu.VMEM((2, span, 2 * LANES), F32),
             pltpu.VMEM((2, head_width // HD, rows), F32),
             pltpu.VMEM((span, 2 * width), F32),
             pltpu.VMEM((2, block, 2 * width), F32),
+            pltpu.VMEM((hops - 1, block, 2 * width), F32),
             pltpu.VMEM((2, hops, block, 2 * width), BF16),
             pltpu.VMEM((2, hops, block, 2 * width), BF16),
             pltpu.VMEM((peers, rows, feats), BF16),
             pltpu.VMEM((feats, peers * rows), BF16),
             pltpu.VMEM((peers, rows, width), BF16),
-            pltpu.VMEM((feats, width), F32),
-            dma((4,)),
-            dma((3, 2)),
+            dma((6,)),
+            dma((1 + REACH, 2)),
             dma((2, hops, 2)),
             dma((2, hops, 2)),
             dma((2, hops)),
@@ -464,12 +515,19 @@
             dma((peers - 1,)),
             dma((peers,)),
             dma((peers,)),
-            dma((1 + feats // (2 * LANES),)),
         ],
         compiler_params=pltpu.CompilerParams(
             collective_id=0, has_side_effects=True, vmem_limit_bytes=48 * 1024 * 1024
         ),
-    )(layer_input, queries, key_heads, value_heads, attn_out, out_grad, log_sums, doc_ids)
+    )(*(pltpu.with_memory_space_constraint(x, pltpu.HBM) for x in (layer_input, queries, key_heads, value_heads, attn_out, out_grad, log_sums, doc_ids)))
+    return pl.pallas_call(
+        store_kernel,
+        out_shape=[jax.ShapeDtypeStruct(result.shape, result.dtype) for result in results],
+        in_specs=[pl.BlockSpec(memory_space=pl.ANY)] * 4,
+        out_specs=[hbm] * 4,
+        scratch_shapes=[dma((4,))],
+        compiler_params=pltpu.CompilerParams(vmem_limit_bytes=1024 * 1024),
+    )(*results)
 
 
 def with_halo(cells, sides, width):

time: 56.1 us -> 44.9 us (0.80)
  local copies, waits for them, and re-layouts: 9.94 us -> 0 us
  Pallas kernels: 45.1 us -> 44.1 us
    unnamed x18 -> x0, local copies, waits for them, and re-layouts: 9.94 us -> none
    pallas_call x1, Pallas kernels: 45.1 us -> 42.7 us  [fused_body(): pl.pallas_call(functools.partial(fused_kernel, sizes), out_shape=(jax.Sha...]
    pallas_call x0 -> x1, Pallas kernels: none -> 1.4 us  [fused_body(): pl.pallas_call(store_kernel, out_shape=[jax.ShapeDtypeStruct(result.shape...]
where the time goes in v1:
time: 44.9 us; the launch traced here: 44.8 us
  Pallas kernels  44.1 us (98%)
  between operations  0.64 us (1%)
    pallas_call x1, Pallas kernels, fused_body(): pl.pallas_call(functools.partial(fused_kernel, sizes), out_shape=(jax.Sha...  42.7 us
    pallas_call x1, Pallas kernels, fused_body(): pl.pallas_call(store_kernel, out_shape=[jax.ShapeDtypeStruct(result.shape...  1.4 us

profile of v1, /device:TPU:0, one launch (start us, length us, event | category | flops | bytes accessed | tf_op | source)
XLA Modules:
  0.0 44.8 jit_solution(8298178527271853826)
XLA Ops:
  0.6 42.7 %shard_map.111 = (bf16[1,128,4096]{2,1,0:T(8,128)(2,1)S(1)}, bf16[1,128,256]{2,1,0:T(8,128)(2,1)S(1)}, bf16[1,128,256]{2,1,0:T(8,128)(2,1)S(1)}, f32[1024,256]{1,0:T(8,128)S(1)}) custom-call(bf16[1,128,8192]{2,1,0:T(8,128)(2,1)} %layer_hbm.1, bf16[1,128,4096]{2,1,0:T(8,128)(2,1)} %q_hbm.1, bf16[1,128,256]{2,1,0:T(8,128)(2,1)} %k_hbm.1, ...), custom_call_target="tpu_custom_call" | custom-call | tf_op jit(solution)/shard_map/pallas_call | solution.py:476
  43.4 1.4 %shard_map.112 = (bf16[1,128,4096]{2,1,0:T(8,128)(2,1)}, bf16[1,128,256]{2,1,0:T(8,128)(2,1)}, bf16[1,128,256]{2,1,0:T(8,128)(2,1)}, f32[1024,256]{1,0:T(8,128)}) custom-call(bf16[1,128,4096]{2,1,0:T(8,128)(2,1)S(1)} %get-tuple-element.8.refs_0_, bf16[1,128,256]{2,1,0:T(8,128)(2,1)S(1)} %get-tuple-element.9.refs_1_, ...), custom_call_target="tpu_custom_call" | custom-call | tf_op jit(solution)/shard_map/pallas_call | solution.py:523
